TPU v7x, 32 devices: a whole 2x2x4 slice. The times are simulated.
32 devices in a mesh: dp: 4 (over y, core), tensor: 8 (over z, x).
Axes of the slice: x: 2, y: 2, z: 4, core: 2. Of those that a mesh axis runs over, the one named last changes fastest.
Arguments:
- hidden_in: bfloat16 [512, 8192], P('dp'), may hold values from -20 to 20
- norm_gain: bfloat16 [8192], replicated, may hold values from 0.25 to 1.75
- q_weight: bfloat16 [8192, 8192], P(None, 'tensor'), as said below
- q_grad: bfloat16 [512, 8192], P('dp', 'tensor'), may hold values from -6 to 6
- q_main: float32 [8192, 8192], P('dp', 'tensor'), may hold values from -6 to 6
- weight_main_gradient: float32 [8192], P('tensor'), may hold values from -6 to 6
Outputs:
- hidden_state_gradient: bfloat16 [512, 8192], P('dp', 'tensor')
- q_main_new: float32 [8192, 8192], P('dp', 'tensor')
- weight_main_updated: float32 [8192], P('tensor')
Inputs may be any that keep to these rules, and one draw needn't show every extreme that they name: `q_weight`: entries of mean 0 and deviation about 8192 ** -0.5.
All inputs are finite; a program needn't handle non-finite values.
Results may differ from a plain program's by a relative error of at most 0.03.
Values may be sent and summed in bfloat16 or wider, within the bound.
A program may use at most 128 MiB of HBM per device.

v0:
```python
import jax
import jax.numpy as jnp
from jax import lax
from jax.sharding import PartitionSpec as P


def body(hidden_in, norm_gain, q_weight, q_grad, q_main, weight_main_gradient):
    hidden_state = hidden_in.astype(jnp.float32)
    inverse_root_mean = lax.rsqrt(
        jnp.mean(hidden_state * hidden_state, axis=-1, keepdims=True) + 1e-05
    )
    normalized_rows = hidden_state * inverse_root_mean
    norm_weight = norm_gain.astype(jnp.float32)
    normalized_input = (normalized_rows * norm_weight).astype(jnp.bfloat16)
    hidden_width = q_weight.shape[1]
    ndp = lax.axis_size("dp")
    owner_start = lax.axis_index("tensor") * hidden_width
    partial_value = lax.dot_general(
        q_grad, q_weight, (((1,), (1,)), ((), ())), preferred_element_type=jnp.float32
    )
    owned_normalized_rows = lax.dynamic_slice_in_dim(normalized_rows, owner_start, hidden_width, 1)
    owned_norm_weight = lax.dynamic_slice_in_dim(norm_weight, owner_start, hidden_width, 0)
    reduced_sum = lax.psum(partial_value.astype(jnp.bfloat16), "tensor").astype(jnp.float32)
    row_statistic = jnp.mean(reduced_sum * norm_weight * normalized_rows, axis=-1, keepdims=True)
    owned_gradient = lax.dynamic_slice_in_dim(reduced_sum, owner_start, hidden_width, 1)
    hidden_state_gradient = (
        inverse_root_mean
        * (owned_gradient * owned_norm_weight - owned_normalized_rows * row_statistic)
    ).astype(jnp.bfloat16)
    weight_contribution = jnp.sum(owned_gradient * owned_normalized_rows, axis=0)
    weight_main_updated = weight_main_gradient + lax.psum(weight_contribution, "dp") / ndp
    product = lax.dot_general(
        normalized_input, q_grad, (((0,), (0,)), ((), ())), preferred_element_type=jnp.float32
    )
    q_main_new = q_main + lax.psum_scatter(
        (product / ndp).astype(jnp.bfloat16), "dp", scatter_dimension=0, tiled=True
    ).astype(jnp.float32)
    return (hidden_state_gradient, q_main_new, weight_main_updated)


def solution(mesh):
    in_specs = (
        P("dp", None),
        P(),
        P(None, "tensor"),
        P("dp", "tensor"),
        P("dp", "tensor"),
        P("tensor"),
    )
    out_specs = (P("dp", "tensor"), P("dp", "tensor"), P("tensor"))
    return jax.shard_map(body, mesh=mesh, in_specs=in_specs, out_specs=out_specs, check_vma=False)
```

profile of v0, /device:TPU:0, one launch (start us, length us, event | category | flops | bytes accessed | tf_op | source)
XLA Modules:
  0.0 176.3 jit_solution(3481527739017991121)
XLA Ops:
  8.0 0.0 copy-start
  8.0 0.0 copy-start.4
  8.0 0.0 copy-start.3
  8.0 0.0 all-reduce.2.cloned.1.call-start
  8.1 0.9 copy-done
  9.0 12.7 %convolution_convert_fusion = bf16[128,8192]{1,0:T(8,128)(2,1)} fusion(bf16[128,1024]{1,0:T(8,128)(2,1)S(1)} %copy-done, bf16[8192,1024]{1,0:T(8,128)(2,1)} %param.8), kind=kOutput, calls=%fused_computation.1 | convolution fusion | flops 2148532224 | bytes 19136512 | tf_op jit(solution)/shard_map/dot_general | solution.py:18
  21.7 0.0 all-reduce.2.cloned.1.call-update
  21.7 0.0 reduce-scatter.2.cloned.1.call-start
  21.7 0.0 copy-done.4
  21.8 0.0 copy-done.3
  21.8 0.5 fusion
  22.3 8.5 %multiply_convert_fusion = bf16[8192,1024]{1,0:T(8,128)(2,1)} fusion(bf16[128,1024]{1,0:T(8,128)(2,1)S(1)} %copy-done, f32[8192]{0:T(1024)S(1)} %convert_element_type.27, bf16[128,8192]{1,0:T(8,128)(2,1)S(1)} %copy-done.3, f32[128]{0:T(128)S(1)} %add_rsqrt_fusion), kind=kOutput, calls=%fused_computation | convolution fusion | flops 2168455168 | bytes 19169792 | tf_op jit(solution)/shard_map/dot_general | solution.py:32
  30.7 0.0 reduce-scatter.2.cloned.1.call-update
  30.8 96.1 %all-reduce.2.cloned.1.call-done = bf16[128,8192]{1,0:T(8,128)(2,1)} async-done(((bf16[128,8192]{1,0:T(8,128)(2,1)}), bf16[128,8192]{1,0:T(8,128)(2,1)}) %all-reduce.2.cloned.1.call-update) | async-done | bytes 2097168 | tf_op jit(solution)/shard_map/psum | solution.py:23
  126.9 0.0 copy-start.2
  126.9 2.1 %convert_element_type.26 = f32[128,8192]{1,0:T(8,128)S(1)} convert(bf16[128,8192]{1,0:T(8,128)(2,1)} %all-reduce.2.cloned.1.call-done) | non-fusion elementwise | flops 1048576 | bytes 6291456 | tf_op jit(solution)/shard_map/convert_element_type | solution.py:23
  129.0 0.1 copy-done.2
  129.1 0.0 copy-start.5
  129.1 1.3 multiply_reduce_fusion
  130.4 0.9 multiply_reduce_fusion.1
  131.2 6.9 %psum.15 = f32[1024]{0:T(1024)S(1)} all-reduce(f32[1024]{0:T(1024)S(1)} %get-tuple-element.3), channel_id=1, replica_groups=mesh['dp'=4,'tensor'=8] {'dp'}, use_global_device_ids=true, to_apply=%region_5.0 | all-reduce | flops 1024 | bytes 8192 | tf_op jit(solution)/shard_map/psum | solution.py:31
  138.2 0.0 copy-done.5
  138.2 0.6 multiply_add_fusion
  138.8 19.8 %reduce-scatter.2.cloned.1.call-done = bf16[2048,1024]{1,0:T(8,128)(2,1)} async-done(((bf16[8192,1024]{1,0:T(8,128)(2,1)}), bf16[2048,1024]{1,0:T(8,128)(2,1)}) %reduce-scatter.2.cloned.1.call-update) | async-done | bytes 4194320 | tf_op jit(solution)/shard_map/reduce_scatter | solution.py:35
  158.6 0.0 copy-start.1
  158.6 10.2 %convert_add_fusion = f32[2048,1024]{1,0:T(8,128)} fusion(f32[2048,1024]{1,0:T(8,128)} %param.10, bf16[2048,1024]{1,0:T(8,128)(2,1)} %reduce-scatter.2.cloned.1.call-done), kind=kLoop, calls=%fused_computation.2 | loop fusion | flops 4194304 | bytes 20971520 | tf_op jit(solution)/shard_map/add | solution.py:35
  168.8 0.0 copy-done.1
  (4 shorter events, 0.0 us)
Async XLA Ops:
  8.0 1.0 copy-start
  8.0 13.7 %copy-start.4 = (bf16[8192]{0:T(1024)(128)(2,1)S(1)}, bf16[8192]{0:T(1024)(128)(2,1)}, u32[]{:S(2)}) copy-start(bf16[8192]{0:T(1024)(128)(2,1)} %param.7) | copy-start | bytes 49156
  8.0 13.7 %copy-start.3 = (bf16[128,8192]{1,0:T(8,128)(2,1)S(1)}, bf16[128,8192]{1,0:T(8,128)(2,1)}, u32[]{:S(2)}) copy-start(bf16[128,8192]{1,0:T(8,128)(2,1)} %param.6) | copy-start | bytes 6291460
  8.0 118.8 %all-reduce.2.cloned.1.call-start = ((), (), s32[]{:S(2)}) async-start(), calls=%async_computation.1 | async-start | bytes 4194304 | tf_op jit(solution)/shard_map/psum | solution.py:23
  21.7 136.9 %reduce-scatter.2.cloned.1.call-start = ((), (), s32[]{:S(2)}) async-start(), calls=%async_computation.2 | async-start | bytes 20971520 | tf_op jit(solution)/shard_map/reduce_scatter | solution.py:35
  126.9 2.2 %copy-start.2 = (bf16[128,8192]{1,0:T(8,128)(2,1)S(1)}, bf16[128,8192]{1,0:T(8,128)(2,1)}, u32[]{:S(2)}) copy-start(bf16[128,8192]{1,0:T(8,128)(2,1)} %all-reduce.2.cloned.1.call-done) | copy-start | bytes 6291460
  129.1 9.1 %copy-start.5 = (f32[1024]{0:T(1024)S(1)}, f32[1024]{0:T(1024)}, u32[]{:S(2)}) copy-start(f32[1024]{0:T(1024)} %param.11) | copy-start | bytes 12292
  158.6 10.2 %copy-start.1 = (bf16[128,1024]{1,0:T(8,128)(2,1)S(1)}, bf16[128,1024]{1,0:T(8,128)(2,1)}, u32[]{:S(2)}) copy-start(bf16[128,1024]{1,0:T(8,128)(2,1)} %param.9) | copy-start | bytes 786436
Sparse Core Ops, SparseCore 0:
  21.8 105.0 all-reduce.1
Sparse Core Ops, SparseCore 1:
  30.9 127.7 reduce-scatter.1
where the time goes:
time: 176 us
  waiting for transfers between devices  116 us (66%)
  matrix products  21.2 us (12%)
  other arithmetic  15.6 us (9%)
  between operations  15.6 us (9%)
  blocking collectives  6.94 us (4%)
    psum x1, waiting for transfers between devices, body(): lax.psum(partial_value.astype(jnp.bfloat16), 'tensor').astype(jnp.float32)  96.1 us
    reduce_scatter x1, waiting for transfers between devices, body(): lax.psum_scatter((product / ndp).astype(jnp.bfloat16), 'dp', scatter_dime...  19.8 us
    dot_general x1, matrix products, body(): lax.dot_general(q_grad, q_weight, (((1,), (1,)), ((), ())), preferred_ele...  12.7 us
    add x1, other arithmetic, body(): q_main + lax.psum_scatter((product / ndp).astype(jnp.bfloat16), 'dp', sca...  10.2 us
    dot_general x1, matrix products, body(): lax.dot_general(normalized_input, q_grad, (((0,), (0,)), ((), ())), prefe...  8.48 us
    psum x1, blocking collectives, body(): lax.psum(weight_contribution, 'dp') / ndp  6.94 us
  transfers between devices with their start and end apart: 2, of which 2 were waited for; matrix products, arithmetic and copies ran while one was open for 8% of the time, Pallas kernels for 0%

commit v1 on v0

v1 whole, which is shorter than its diff:
```python
import functools

import jax
import jax.numpy as jnp
from jax import lax
from jax.experimental import pallas as pl
from jax.experimental.pallas import tpu as pltpu
from jax.sharding import PartitionSpec as P

MESH = pl.DeviceIdType.MESH
F32 = jnp.float32
BF16 = jnp.bfloat16
NT_DIMS = (((1,), (1,)), ((), ()))


def kernel(
    ndp, nt,
    hid, gain, qg, w_hbm, wmg,
    hsg, hg, gg, wmu,
    wbuf, own, xsend, xrecv, zsend, zrecv, gs, stat_acc, ssend, srecv, wsend, wrecv,
    wsem, lsem, xs, xr, zs, zr, hs, hr, gsnd, grcv, ss, sr, ws, wr,
):
    tokens, width = hid.shape
    chunk = width // nt
    rows = width // ndp
    no, ny = nt // 2, ndp // 2
    p, t = lax.axis_index("dp"), lax.axis_index("tensor")
    y, c = p // 2, p % 2
    o, x = t // 2, t % 2
    xpeer = o * 2 + (1 - x)

    def remote(src, dst, send, recv, dev_p, dev_t):
        return pltpu.make_async_remote_copy(
            src_ref=src, dst_ref=dst, send_sem=send, recv_sem=recv,
            device_id=(dev_p, dev_t), device_id_type=MESH)

    barrier = pltpu.get_barrier_semaphore()
    for k in range(1, nt):
        pl.semaphore_signal(barrier, inc=1, device_id=(p, (t + k) % nt), device_id_type=MESH)
    for k in range(1, ndp):
        pl.semaphore_signal(barrier, inc=1, device_id=((p + k) % ndp, t), device_id_type=MESH)

    targets = [(o + s + 1) % no for s in range(no)]
    order = [targets[s] * 2 + (1 - x) for s in range(no)] + [targets[s] * 2 + x for s in range(no)]
    loads = []
    for i in range(nt):
        load = pltpu.make_async_copy(
            w_hbm.at[pl.ds(pl.multiple_of(order[i] * chunk, chunk), chunk), :], wbuf.at[i], wsem.at[i])
        load.start()
        loads.append(load)

    def peer(j):
        ky, cc = j // 2, j % 2
        return ((y + ky) % ny) * 2 + ((c + cc) % 2)

    def hid_cols(q):
        return hid.at[:, pl.ds(pl.multiple_of(q * rows, rows), rows)]

    local_h = pltpu.make_async_copy(hid_cols(p), hg.at[0], lsem.at[0])
    local_h.start()
    pl.semaphore_wait(barrier, nt - 1 + ndp - 1)

    hcopies = {}
    for j in list(range(3, ndp, 2)) + [1]:
        hcopies[j] = remote(hid_cols(peer(j)), hg.at[j], hs.at[j], hr.at[j], peer(j), t)
        hcopies[j].start()

    step_w = min(512, width)

    def square(i, total):
        v = hid[:, pl.ds(pl.multiple_of(i * step_w, step_w), step_w)].astype(F32)
        v = v * v
        for k in range(step_w // 128):
            total = total + v[:, k * 128:(k + 1) * 128]
        return total

    total = lax.fori_loop(0, width // step_w, square, jnp.zeros((tokens, 128), F32))
    rinv = lax.rsqrt(jnp.sum(total, axis=1, keepdims=True) / width + 1e-05)
    gs[...] = (qg[...].astype(F32) * rinv).astype(BF16)
    local_g = pltpu.make_async_copy(gs, gg.at[0], lsem.at[1])
    local_g.start()
    gcopies = {}
    for j in list(range(2, ndp, 2)) + [1]:
        gcopies[j] = remote(gs, gg.at[j], gsnd.at[j], grcv.at[j], peer(j), t)
        gcopies[j].start()
    for j in range(2, ndp, 2):
        hcopies[j] = remote(hid_cols(peer(j)), hg.at[j], hs.at[j], hr.at[j], peer(j), t)
        hcopies[j].start()

    stat_acc[...] = jnp.zeros_like(stat_acc)
    tile = min(256, chunk)

    def compute(i, store):
        loads[i].wait()

        @pl.loop(0, chunk // tile)
        def _(n):
            at = pl.multiple_of(n * tile, tile)
            part = lax.dot_general(
                qg[...], wbuf[i, pl.ds(at, tile), :], NT_DIMS, preferred_element_type=F32)
            store(at, part)
            cols = pl.ds(pl.multiple_of(order[i] * chunk + at, tile), tile)
            v = part * gain[:, cols].astype(F32) * hid[:, cols].astype(F32)
            for k in range(tile // 128):
                stat_acc[...] += v[:, k * 128:(k + 1) * 128]

    xcopies = []
    for s in range(no):
        def put(at, part, s=s):
            xsend[s, :, pl.ds(at, tile)] = part.astype(BF16)
        compute(s, put)
        copy = remote(xsend.at[s], xrecv.at[s], xs.at[s], xr.at[s], p, xpeer)
        copy.start()
        xcopies.append(copy)
    for s in range(no):
        def put(at, part, s=s):
            own[s, :, pl.ds(at, tile)] = part
        compute(no + s, put)

    mine = jnp.sum((stat_acc[...] * (rinv / width)).T, axis=0, keepdims=True)
    ssend[...] = jnp.broadcast_to(mine, ssend.shape)
    scopies = []
    for k in range(1, nt):
        copy = remote(ssend, srecv.at[k], ss.at[k], sr.at[k], p, (t + k) % nt)
        copy.start()
        scopies.append(copy)

    zcopies = []
    for s in range(no - 1):
        xcopies[s].wait_recv()
        zsend[s] = (own[s] + xrecv[s].astype(F32)).astype(BF16)
        copy = remote(zsend.at[s], zrecv.at[s], zs.at[s], zr.at[s], p, targets[s] * 2 + x)
        copy.start()
        zcopies.append(copy)

    rcopies = {}
    for j in range(2, ndp, 2):
        gcopies[j].wait_recv()
        rcopies[j + 1] = remote(gg.at[j], gg.at[j + 1], gsnd.at[j + 1], grcv.at[j + 1], y * 2 + (1 - c), t)
        rcopies[j + 1].start()

    xcopies[no - 1].wait_recv()
    ng = own[no - 1] + xrecv[no - 1].astype(F32)
    for s in range(no - 1):
        zcopies[s].wait_recv()
        ng = ng + zrecv[s].astype(F32)
    own[0] = ng
    mycols = pl.ds(pl.multiple_of(t * chunk, chunk), chunk)
    xhat = hid[:, mycols].astype(F32) * rinv
    contribution = jnp.sum(own[0] * xhat, axis=0, keepdims=True)
    wsend[...] = jnp.broadcast_to(contribution, wsend.shape)
    wcopies = []
    for k in range(1, ndp):
        copy = remote(wsend, wrecv.at[k], ws.at[k], wr.at[k], (p + k) % ndp, t)
        copy.start()
        wcopies.append(copy)

    stat = mine
    for k in range(1, nt):
        scopies[k - 1].wait_recv()
        stat = stat + srecv[k, 0:1, :]
    stat_col = jnp.broadcast_to(stat, (tokens, tokens)).T[:, 0:1]
    hsg[...] = (rinv * (own[0] * gain[:, mycols].astype(F32) - xhat * stat_col)).astype(BF16)

    weight = wsend[0:1, :]
    for k in range(1, ndp):
        wcopies[k - 1].wait_recv()
        weight = weight + wrecv[k, 0:1, :]
    wmu[...] = wmg[...] + weight / ndp

    for copy in rcopies.values():
        copy.wait_recv()
    gcopies[1].wait_recv()
    for copy in hcopies.values():
        copy.wait_recv()
    local_h.wait()
    local_g.wait()
    for copy in (*xcopies, *zcopies, *scopies, *wcopies, *gcopies.values(), *rcopies.values(), *hcopies.values()):
        copy.wait_send()


def body(ndp, nt, hidden_in, norm_gain, q_weight, q_grad, q_main, weight_main_gradient):
    tokens, width = hidden_in.shape
    features = q_weight.shape[1]
    chunk, rows, no = width // nt, width // ndp, nt // 2
    vmem = pl.BlockSpec(memory_space=pltpu.VMEM)
    anywhere = pl.BlockSpec(memory_space=pl.ANY)
    dma = pltpu.SemaphoreType.DMA
    hsg, hg, gg, wmu = pl.pallas_call(
        functools.partial(kernel, ndp, nt),
        out_shape=(
            jax.ShapeDtypeStruct((tokens, chunk), BF16),
            jax.ShapeDtypeStruct((ndp, tokens, rows), BF16),
            jax.ShapeDtypeStruct((ndp, tokens, features), BF16),
            jax.ShapeDtypeStruct((1, chunk), F32),
        ),
        in_specs=[vmem, vmem, vmem, anywhere, vmem],
        out_specs=(vmem, anywhere, anywhere, vmem),
        scratch_shapes=[
            pltpu.VMEM((nt, chunk, features), BF16),
            pltpu.VMEM((no, tokens, chunk), F32),
            pltpu.VMEM((no, tokens, chunk), BF16),
            pltpu.VMEM((no, tokens, chunk), BF16),
            pltpu.VMEM((no, tokens, chunk), BF16),
            pltpu.VMEM((no, tokens, chunk), BF16),
            pltpu.VMEM((tokens, features), BF16),
            pltpu.VMEM((tokens, 128), F32),
            pltpu.VMEM((8, tokens), F32),
            pltpu.VMEM((nt, 8, tokens), F32),
            pltpu.VMEM((8, chunk), F32),
            pltpu.VMEM((ndp, 8, chunk), F32),
            dma((nt,)), dma((2,)),
            dma((no,)), dma((no,)), dma((no,)), dma((no,)),
            dma((ndp,)), dma((ndp,)), dma((ndp,)), dma((ndp,)),
            dma((nt,)), dma((nt,)), dma((ndp,)), dma((ndp,)),
        ],
        compiler_params=pltpu.CompilerParams(
            collective_id=0, has_side_effects=True, vmem_limit_bytes=56 * 1024 * 1024),
    )(hidden_in, norm_gain.reshape(1, width), q_grad, q_weight, weight_main_gradient.reshape(1, chunk))
    product = lax.dot_general(
        hg.reshape(ndp * tokens, rows), gg.reshape(ndp * tokens, features),
        (((0,), (0,)), ((), ())), preferred_element_type=F32)
    gain_rows = lax.dynamic_slice_in_dim(norm_gain, lax.axis_index("dp") * rows, rows, 0)
    q_main_new = q_main + product * (gain_rows.astype(F32) / ndp)[:, None]
    return hsg, q_main_new, wmu.reshape(chunk)


def solution(mesh):
    ndp, nt = mesh.shape["dp"], mesh.shape["tensor"]
    in_specs = (
        P("dp", None),
        P(),
        P(None, "tensor"),
        P("dp", "tensor"),
        P("dp", "tensor"),
        P("tensor"),
    )
    out_specs = (P("dp", "tensor"), P("dp", "tensor"), P("tensor"))
    return jax.shard_map(
        functools.partial(body, ndp, nt), mesh=mesh, in_specs=in_specs, out_specs=out_specs, check_vma=False)
```

time: 176 us -> 59.9 us (0.34)
  the two profiles are of different devices: /device:TPU:0 before, /device:TPU:9 now
where the time goes in v1:
time: 59.9 us; the launch traced here: 59.6 us
  Pallas kernels  45.4 us (76%)
  matrix products  10.2 us (17%)
  local copies, waits for them, and re-layouts  2.65 us (4%)
  other arithmetic  0.69 us (1%)
  between operations  0.66 us (1%)
    pallas_call x1, Pallas kernels, body(): pl.pallas_call(functools.partial(kernel, ndp, nt), out_shape=(jax.ShapeDt...  45.4 us
    dot_general x1, matrix products, body(): lax.dot_general(hg.reshape(ndp * tokens, rows), gg.reshape(ndp * tokens,...  10.2 us
    reshape x1, local copies, waits for them, and re-layouts, body(): norm_gain.reshape(1, width)  1.35 us
    unnamed x6, local copies, waits for them, and re-layouts  1.3 us

profile of v1, /device:TPU:9, one launch (start us, length us, event | category | flops | bytes accessed | tf_op | source)
XLA Modules:
  0.0 59.6 jit_solution(16320285974131186850)
XLA Ops:
  0.6 0.7 %convert_multiply_fusion = f32[2048]{0:T(1024)S(1)} fusion(bf16[8192]{0:T(1024)(128)(2,1)} %param.7, s32[]{:T(128)S(6)} %select_n.3), kind=kLoop, calls=%fused_computation.2 | loop fusion | flops 4096 | bytes 12292 | tf_op jit(solution)/shard_map/div | solution.py:224
  1.3 1.3 %reshape.18.gain = bf16[1,8192]{1,0:T(2,128)(2,1)} reshape(bf16[8192]{0:T(1024)(128)(2,1)} %param.7) | data formatting | bytes 32768 | tf_op jit(solution)/shard_map/reshape | solution.py:219
  2.7 45.4 %shard_map.85 = (bf16[128,1024]{1,0:T(8,128)(2,1)}, bf16[4,128,2048]{2,1,0:T(8,128)(2,1)}, bf16[4,128,1024]{2,1,0:T(8,128)(2,1)}, f32[1,1024]{1,0:T(1,128)}) custom-call(bf16[128,8192]{1,0:T(8,128)(2,1)} %hid.1, bf16[1,8192]{1,0:T(2,128)(2,1)} %reshape.18.gain, bf16[128,1024]{1,0:T(8,128)(2,1)} %qg.1, bf16[8192,1024]{1,0:T(8,128)(2,1)} %w_hbm.1, ...), custom_call_target="tpu_custom_call" | custom-call | tf_op jit(solution)/shard_map/pallas_call | solution.py:189
  48.1 0.0 copy-start
  48.1 0.0 copy-start.1
  48.1 10.2 %fusion = f32[2048,1024]{1,0:T(8,128)} fusion(f32[2048,1024]{1,0:T(8,128)} %param.10, bf16[4,128,2048]{2,1,0:T(8,128)(2,1)} %get-tuple-element.8, bf16[4,128,1024]{2,1,0:T(8,128)(2,1)} %get-tuple-element.9, f32[2048]{0:T(1024)S(1)} %convert_multiply_fusion), kind=kOutput, calls=%fused_computation.1 | convolution fusion | flops 2151677952 | bytes 19931136 | tf_op jit(solution)/shard_map/dot_general | solution.py:220
  58.3 0.0 copy-done
  58.3 0.7 %copy.13 = bf16[128,1024]{1,0:T(8,128)(2,1)} copy(bf16[128,1024]{1,0:T(8,128)(2,1)S(1)} %copy-done) | data formatting | bytes 524288
  59.0 0.0 copy-done.1
  59.0 0.6 copy.14
Async XLA Ops:
  48.1 10.2 %copy-start = (bf16[128,1024]{1,0:T(8,128)(2,1)S(1)}, bf16[128,1024]{1,0:T(8,128)(2,1)}, u32[]{:S(2)}) copy-start(bf16[128,1024]{1,0:T(8,128)(2,1)} %get-tuple-element.14) | copy-start | bytes 786436
  48.1 10.9 %copy-start.1 = (f32[1,1024]{1,0:T(1,128)S(1)}, f32[1,1024]{1,0:T(1,128)}, u32[]{:S(2)}) copy-start(f32[1,1024]{1,0:T(1,128)} %get-tuple-element.10) | copy-start | bytes 12292

commit v2 on v1

v2 whole, which is shorter than its diff:
```python
import functools

import jax
import jax.numpy as jnp
from jax import lax
from jax.experimental import pallas as pl
from jax.experimental.pallas import tpu as pltpu
from jax.sharding import PartitionSpec as P

MESH = pl.DeviceIdType.MESH
F32 = jnp.float32
BF16 = jnp.bfloat16
NT_DIMS = (((1,), (1,)), ((), ()))


PARTS = 2
SLOTS = 8
VMEM_MIB = 28


def kernel(
    ndp, nt,
    hid_hbm, gain_in, qg, w_hbm, wmg,
    hsg, hg, gg, wmu, gout,
    hid, gain, wbuf, own, xsend, xrecv, zsend, zrecv, gs, stat_acc, ssend, srecv, wsend, wrecv,
    wsem, lsem, xs, xr, zs, zr, hs, hr, gsnd, grcv, ss, sr, ws, wr,
):
    tokens, width = hid.shape
    chunk = width // nt
    piece = chunk // PARTS
    rows = width // ndp
    no, ny = nt // 2, ndp // 2
    p, t = lax.axis_index("dp"), lax.axis_index("tensor")
    y, c = p // 2, p % 2
    o, x = t // 2, t % 2
    xpeer = o * 2 + (1 - x)

    def remote(src, dst, send, recv, dev_p, dev_t):
        copy = pltpu.make_async_remote_copy(
            src_ref=src, dst_ref=dst, send_sem=send, recv_sem=recv,
            device_id=(dev_p, dev_t), device_id_type=MESH)
        copy.start()
        return copy

    barrier = pltpu.get_barrier_semaphore()
    for k in range(1, nt):
        pl.semaphore_signal(barrier, inc=1, device_id=(p, (t + k) % nt), device_id_type=MESH)
    for k in range(1, ndp):
        pl.semaphore_signal(barrier, inc=1, device_id=((p + k) % ndp, t), device_id_type=MESH)

    def flip(k):
        value, bit = o, 1
        while bit < no:
            if k & bit:
                value = value + bit - 2 * bit * ((o // bit) % 2)
            bit *= 2
        return value

    units = [(k, h) for k in range(no - 1, -1, -1) for h in range(PARTS)]
    away = [(k, h, 1) for k, h in units]
    home = [(k, h, 0) for k, h in units]
    plan = away[:2]
    for i in range(len(units)):
        plan.append(home[i])
        if i + 2 < len(units):
            plan.append(away[i + 2])

    def column(unit):
        k, h, far = unit
        side = (1 - x) if far else x
        return pl.multiple_of((flip(k) * 2 + side) * chunk + h * piece, piece)

    loads = {}

    def load(i):
        if i < len(plan):
            loads[i] = pltpu.make_async_copy(
                w_hbm.at[pl.ds(column(plan[i]), piece), :], wbuf.at[i % SLOTS], wsem.at[i % SLOTS])
            loads[i].start()

    load(0)
    load_h = pltpu.make_async_copy(hid_hbm, hid, lsem.at[2])
    load_h.start()
    for i in range(1, 4):
        load(i)

    def peer(j):
        ky, cc = j // 2, j % 2
        return ((y + ky) % ny) * 2 + ((c + cc) % 2)

    def hid_cols(ref, q):
        return ref.at[:, pl.ds(pl.multiple_of(q * rows, rows), rows)]

    gain[...] = gain_in[...].astype(F32)
    pl.semaphore_wait(barrier, nt - 1 + ndp - 1)

    hcopies, gcopies, rcopies = {}, {}, {}

    def send_hidden(j):
        hcopies[j] = remote(hid_cols(hid_hbm, peer(j)), hg.at[j], hs.at[j], hr.at[j], peer(j), t)

    for j in range(3, ndp, 2):
        send_hidden(j)

    stat_acc[...] = jnp.zeros_like(stat_acc)
    tile = min(256, piece)
    xcopies, zcopies = {}, {}

    def compute(i):
        k, h, far = plan[i]
        loads[i].wait()
        base = column(plan[i])

        @pl.loop(0, piece // tile)
        def _(n):
            at = pl.multiple_of(n * tile, tile)
            part = lax.dot_general(
                qg[...], wbuf[i % SLOTS, pl.ds(at, tile), :], NT_DIMS, preferred_element_type=F32)
            if far:
                xsend[k, h, :, pl.ds(at, tile)] = part.astype(BF16)
            else:
                own[k, h, :, pl.ds(at, tile)] = part
            for m in range(tile // 128):
                cols = pl.ds(pl.multiple_of(base + at + m * 128, 128), 128)
                line = gain[pl.ds((base + at) // 128 + m, 1), :]
                stat_acc[...] += part[:, m * 128:(m + 1) * 128] * line * hid[:, cols].astype(F32)

        load(i + 4)
        if far:
            xcopies[k, h] = remote(xsend.at[k, h], xrecv.at[k, h], xs.at[k, h], xr.at[k, h], p, xpeer)

    def reduce(k, h):
        xcopies[k, h].wait_recv()
        total = own[k, h] + xrecv[k, h].astype(F32)
        low = k & -k if k else no
        bit = 1
        while bit < low:
            zcopies[k + bit, h].wait_recv()
            total = total + zrecv[k + bit, h].astype(F32)
            bit *= 2
        if k:
            zsend[k, h] = total.astype(BF16)
            zcopies[k, h] = remote(
                zsend.at[k, h], zrecv.at[k, h], zs.at[k, h], zr.at[k, h], p, flip(low) * 2 + x)
        else:
            own[0, h] = total

    load_h.wait()
    compute(0)
    compute(1)

    step_w = min(512, width)

    def square(i, total):
        v = hid[:, pl.ds(pl.multiple_of(i * step_w, step_w), step_w)].astype(F32)
        v = v * v
        for k in range(step_w // 128):
            total = total + v[:, k * 128:(k + 1) * 128]
        return total

    total = lax.fori_loop(0, width // step_w, square, jnp.zeros((tokens, 128), F32))
    rinv = lax.rsqrt(jnp.sum(total, axis=1, keepdims=True) / width + 1e-05)
    gs[...] = (qg[...].astype(F32) * rinv).astype(BF16)
    for j in list(range(2, ndp, 2)) + [1]:
        gcopies[j] = remote(gs, gg.at[j], gsnd.at[j], grcv.at[j], peer(j), t)
    for j in list(range(2, ndp, 2)) + [1]:
        send_hidden(j)
    local_g = pltpu.make_async_copy(gs, gg.at[0], lsem.at[1])
    local_g.start()
    local_h = pltpu.make_async_copy(hid_cols(hid, p), hg.at[0], lsem.at[0])
    local_h.start()
    gout[...] = gain[pl.ds(pl.multiple_of(p * (rows // 128), rows // 128), rows // 128), :] / ndp

    done = 0
    for i in range(2, len(plan)):
        compute(i)
        if i in (8, 12) and done < PARTS and i < len(plan) - 1:
            reduce(*units[done])
            done += 1

    mine = jnp.sum((stat_acc[...] * (rinv / width)).T, axis=0, keepdims=True)
    ssend[...] = jnp.broadcast_to(mine, ssend.shape)
    scopies = {}
    for k in range(1, nt):
        scopies[k] = remote(ssend, srecv.at[k], ss.at[k], sr.at[k], p, (t + k) % nt)

    for unit in units[done:-PARTS]:
        reduce(*unit)

    for j in range(2, ndp, 2):
        gcopies[j].wait_recv()
        rcopies[j + 1] = remote(gg.at[j], gg.at[j + 1], gsnd.at[j + 1], grcv.at[j + 1], y * 2 + (1 - c), t)

    stat = mine
    for k in range(1, nt):
        scopies[k].wait_recv()
        stat = stat + srecv[k, 0:1, :]
    stat_col = jnp.broadcast_to(stat, (tokens, tokens)).T[:, 0:1]

    for h in range(PARTS):
        reduce(0, h)
        mycols = pl.ds(pl.multiple_of(t * chunk + h * piece, piece), piece)
        xhat = hid[:, mycols].astype(F32) * rinv
        contribution = jnp.sum(own[0, h] * xhat, axis=0, keepdims=True)
        wsend[:, h * piece:(h + 1) * piece] = jnp.broadcast_to(contribution, (8, piece))
    wcopies = {}
    for k in range(1, ndp):
        wcopies[k] = remote(wsend, wrecv.at[k], ws.at[k], wr.at[k], (p + k) % ndp, t)
    for h in range(PARTS):
        for m in range(piece // 128):
            part_cols = slice(m * 128, (m + 1) * 128)
            at = t * chunk + h * piece + m * 128
            line = gain[pl.ds(at // 128, 1), :]
            xhat = hid[:, pl.ds(pl.multiple_of(at, 128), 128)].astype(F32) * rinv
            value = rinv * (own[0, h, :, part_cols] * line - xhat * stat_col)
            hsg[:, h * piece + m * 128:h * piece + (m + 1) * 128] = value.astype(BF16)

    weight = wsend[0:1, :]
    for k in range(1, ndp):
        wcopies[k].wait_recv()
        weight = weight + wrecv[k, 0:1, :]
    wmu[...] = wmg[...] + weight / ndp

    for copies in (rcopies, hcopies):
        for copy in copies.values():
            copy.wait_recv()
    gcopies[1].wait_recv()
    local_h.wait()
    local_g.wait()
    for copies in (xcopies, zcopies, scopies, wcopies, gcopies, rcopies, hcopies):
        for copy in copies.values():
            copy.wait_send()


def body(ndp, nt, hidden_in, norm_gain, q_weight, q_grad, q_main, weight_main_gradient):
    tokens, width = hidden_in.shape
    features = q_weight.shape[1]
    chunk, rows, no = width // nt, width // ndp, nt // 2
    vmem = pl.BlockSpec(memory_space=pltpu.VMEM)
    anywhere = pl.BlockSpec(memory_space=pl.ANY)
    hbm = pl.BlockSpec(memory_space=pltpu.HBM)
    dma = pltpu.SemaphoreType.DMA
    piece = chunk // PARTS
    hsg, hg, gg, wmu, gout = pl.pallas_call(
        functools.partial(kernel, ndp, nt),
        out_shape=(
            jax.ShapeDtypeStruct((tokens, chunk), BF16),
            jax.ShapeDtypeStruct((ndp, tokens, rows), BF16),
            jax.ShapeDtypeStruct((ndp, tokens, features), BF16),
            jax.ShapeDtypeStruct((1, chunk), F32),
            jax.ShapeDtypeStruct((rows // 128, 128), F32),
        ),
        in_specs=[hbm, vmem, vmem, hbm, vmem],
        out_specs=(vmem, anywhere, anywhere, vmem, vmem),
        scratch_shapes=[
            pltpu.VMEM((tokens, width), BF16),
            pltpu.VMEM((width // 128, 128), F32),
            pltpu.VMEM((SLOTS, piece, features), BF16),
            pltpu.VMEM((no, PARTS, tokens, piece), F32),
            pltpu.VMEM((no, PARTS, tokens, piece), BF16),
            pltpu.VMEM((no, PARTS, tokens, piece), BF16),
            pltpu.VMEM((no, PARTS, tokens, piece), BF16),
            pltpu.VMEM((no, PARTS, tokens, piece), BF16),
            pltpu.VMEM((tokens, features), BF16),
            pltpu.VMEM((tokens, 128), F32),
            pltpu.VMEM((8, tokens), F32),
            pltpu.VMEM((nt, 8, tokens), F32),
            pltpu.VMEM((8, chunk), F32),
            pltpu.VMEM((ndp, 8, chunk), F32),
            dma((SLOTS,)), dma((3,)),
            dma((no, PARTS)), dma((no, PARTS)), dma((no, PARTS)), dma((no, PARTS)),
            dma((ndp,)), dma((ndp,)), dma((ndp,)), dma((ndp,)),
            dma((nt,)), dma((nt,)), dma((ndp,)), dma((ndp,)),
        ],
        compiler_params=pltpu.CompilerParams(
            collective_id=0, has_side_effects=True, vmem_limit_bytes=VMEM_MIB * 1024 * 1024),
    )(hidden_in, norm_gain.reshape(width // 128, 128), q_grad, q_weight, weight_main_gradient.reshape(1, chunk))
    product = lax.dot_general(
        hg.reshape(ndp * tokens, rows), gg.reshape(ndp * tokens, features),
        (((0,), (0,)), ((), ())), preferred_element_type=F32)
    q_main_new = q_main + product * gout.reshape(rows)[:, None]
    return hsg, q_main_new, wmu.reshape(chunk)


def solution(mesh):
    ndp, nt = mesh.shape["dp"], mesh.shape["tensor"]
    in_specs = (
        P("dp", None),
        P(),
        P(None, "tensor"),
        P("dp", "tensor"),
        P("dp", "tensor"),
        P("tensor"),
    )
    out_specs = (P("dp", "tensor"), P("dp", "tensor"), P("tensor"))
    return jax.shard_map(
        functools.partial(body, ndp, nt), mesh=mesh, in_specs=in_specs, out_specs=out_specs, check_vma=False)
```

time: 59.9 us -> 56.3 us (0.940)
  the two profiles are of different devices: /device:TPU:9 before, /device:TPU:0 now
where the time goes in v2:
time: 56.3 us; the launch traced here: 56 us
  Pallas kernels  38.5 us (68%)
  local copies, waits for them, and re-layouts  11 us (20%)
  matrix products  5.81 us (10%)
  between operations  0.66 us (1%)
    pallas_call x1, Pallas kernels, body(): pl.pallas_call(functools.partial(kernel, ndp, nt), out_shape=(jax.ShapeDt...  38.5 us
    unnamed x14, local copies, waits for them, and re-layouts  11 us
    dot_general x1, matrix products, body(): lax.dot_general(hg.reshape(ndp * tokens, rows), gg.reshape(ndp * tokens,...  5.81 us

profile of v2, /device:TPU:0, one launch (start us, length us, event | category | flops | bytes accessed | tf_op | source)
XLA Modules:
  0.0 56.0 jit_solution(6029354708121347061)
XLA Ops:
  0.6 0.0 copy-start
  0.6 5.8 %copy-done = bf16[8192,1024]{1,0:T(8,128)(2,1)S(1)} copy-done((bf16[8192,1024]{1,0:T(8,128)(2,1)S(1)}, bf16[8192,1024]{1,0:T(8,128)(2,1)}, u32[]{:S(2)}) %copy-start) | copy-done | bytes 16777240
  6.4 0.0 copy-start.1
  6.4 1.6 %copy-done.1 = bf16[128,8192]{1,0:T(8,128)(2,1)S(1)} copy-done((bf16[128,8192]{1,0:T(8,128)(2,1)S(1)}, bf16[128,8192]{1,0:T(8,128)(2,1)}, u32[]{:S(2)}) %copy-start.1) | copy-done | bytes 2097176
  8.0 0.0 copy-start.2
  8.0 0.9 %copy-done.2 = bf16[128,1024]{1,0:T(8,128)(2,1)S(1)} copy-done((bf16[128,1024]{1,0:T(8,128)(2,1)S(1)}, bf16[128,1024]{1,0:T(8,128)(2,1)}, u32[]{:S(2)}) %copy-start.2) | copy-done | bytes 262168
  8.9 0.0 copy-start.3
  8.9 0.7 %copy-done.3 = bf16[8192]{0:T(1024)(128)(2,1)S(1)} copy-done((bf16[8192]{0:T(1024)(128)(2,1)S(1)}, bf16[8192]{0:T(1024)(128)(2,1)}, u32[]{:S(2)}) %copy-start.3) | copy-done | bytes 16408
  9.7 0.0 copy-start.4
  9.7 0.7 %copy-done.4 = f32[1024]{0:T(1024)S(1)} copy-done((f32[1024]{0:T(1024)S(1)}, f32[1024]{0:T(1024)}, u32[]{:S(2)}) %copy-start.4) | copy-done | bytes 4120
  10.3 0.0 copy-start.5
  10.4 38.5 %shard_map.85 = (bf16[128,1024]{1,0:T(8,128)(2,1)S(1)}, bf16[4,128,2048]{2,1,0:T(8,128)(2,1)S(1)}, bf16[4,128,1024]{2,1,0:T(8,128)(2,1)S(1)}, f32[1,1024]{1,0:T(1,128)S(1)}, f32[16,128]{1,0:T(8,128)S(1)}) custom-call(bf16[128,8192]{1,0:T(8,128)(2,1)S(1)} %copy-done.1, bf16[64,128]{1,0:T(8,128)(2,1)S(1)} %bitcast.11, bf16[128,1024]{1,0:T(8,128)(2,1)S(1)} %copy-done.2, ...), custom_call_target="tpu_custom_call" | custom-call | tf_op jit(solution)/shard_map/pallas_call | solution.py:244
  48.9 0.0 copy-done.5
  48.9 5.8 %fusion = f32[2048,1024]{1,0:T(8,128)} fusion(f32[2048,1024]{1,0:T(8,128)S(1)} %copy-done.5, bf16[4,128,2048]{2,1,0:T(8,128)(2,1)S(1)} %get-tuple-element.9, bf16[4,128,1024]{2,1,0:T(8,128)(2,1)S(1)} %get-tuple-element.10, f32[2048]{0:T(1024)S(1)} %bitcast.10), kind=kOutput, calls=%fused_computation.1 | convolution fusion | flops 2151677952 | bytes 19931136 | tf_op jit(solution)/shard_map/dot_general | solution.py:278
  54.7 0.7 %copy.13 = bf16[128,1024]{1,0:T(8,128)(2,1)} copy(bf16[128,1024]{1,0:T(8,128)(2,1)S(1)} %get-tuple-element.16) | data formatting | bytes 524288
  55.4 0.6 %copy.14 = f32[1024]{0:T(1024)} copy(f32[1024]{0:T(1024)S(1)} %bitcast.13) | data formatting | bytes 8192
Async XLA Ops:
  0.6 5.8 %copy-start = (bf16[8192,1024]{1,0:T(8,128)(2,1)S(1)}, bf16[8192,1024]{1,0:T(8,128)(2,1)}, u32[]{:S(2)}) copy-start(bf16[8192,1024]{1,0:T(8,128)(2,1)} %w_hbm.1) | copy-start | bytes 50331652
  6.4 1.6 %copy-start.1 = (bf16[128,8192]{1,0:T(8,128)(2,1)S(1)}, bf16[128,8192]{1,0:T(8,128)(2,1)}, u32[]{:S(2)}) copy-start(bf16[128,8192]{1,0:T(8,128)(2,1)} %hid_hbm.1) | copy-start | bytes 6291460
  8.0 0.9 %copy-start.2 = (bf16[128,1024]{1,0:T(8,128)(2,1)S(1)}, bf16[128,1024]{1,0:T(8,128)(2,1)}, u32[]{:S(2)}) copy-start(bf16[128,1024]{1,0:T(8,128)(2,1)} %qg.1) | copy-start | bytes 786436
  8.9 0.7 %copy-start.3 = (bf16[8192]{0:T(1024)(128)(2,1)S(1)}, bf16[8192]{0:T(1024)(128)(2,1)}, u32[]{:S(2)}) copy-start(bf16[8192]{0:T(1024)(128)(2,1)} %param.7) | copy-start | bytes 49156
  9.7 0.7 %copy-start.4 = (f32[1024]{0:T(1024)S(1)}, f32[1024]{0:T(1024)}, u32[]{:S(2)}) copy-start(f32[1024]{0:T(1024)} %param.11) | copy-start | bytes 12292
  10.3 38.5 %copy-start.5 = (f32[2048,1024]{1,0:T(8,128)S(1)}, f32[2048,1024]{1,0:T(8,128)}, u32[]{:S(2)}) copy-start(f32[2048,1024]{1,0:T(8,128)} %param.10) | copy-start | bytes 25165828

commit v3 on v2

--- a/solution.py
+++ b/solution.py
@@ -15,14 +15,14 @@
 
 PARTS = 2
 SLOTS = 8
-VMEM_MIB = 28
+VMEM_KIB = 51200
 
 
 def kernel(
     ndp, nt,
-    hid_hbm, gain_in, qg, w_hbm, wmg,
+    hid_hbm, gain_hbm, qg_hbm, w_hbm,
     hsg, hg, gg, wmu, gout,
-    hid, gain, wbuf, own, xsend, xrecv, zsend, zrecv, gs, stat_acc, ssend, srecv, wsend, wrecv,
+    hid, gain_in, qg, gain, wbuf, own, xsend, xrecv, zsend, zrecv, gs, stat_acc, ssend, srecv, wsend, wrecv,
     wsem, lsem, xs, xr, zs, zr, hs, hr, gsnd, grcv, ss, sr, ws, wr,
 ):
     tokens, width = hid.shape
@@ -79,6 +79,10 @@
             loads[i].start()
 
     load(0)
+    small = []
+    for i, (src, dst) in enumerate(((qg_hbm, qg), (gain_hbm, gain_in))):
+        small.append(pltpu.make_async_copy(src, dst, lsem.at[3 + i]))
+        small[-1].start()
     load_h = pltpu.make_async_copy(hid_hbm, hid, lsem.at[2])
     load_h.start()
     for i in range(1, 4):
@@ -91,7 +95,6 @@
     def hid_cols(ref, q):
         return ref.at[:, pl.ds(pl.multiple_of(q * rows, rows), rows)]
 
-    gain[...] = gain_in[...].astype(F32)
     pl.semaphore_wait(barrier, nt - 1 + ndp - 1)
 
     hcopies, gcopies, rcopies = {}, {}, {}
@@ -145,6 +148,9 @@
         else:
             own[0, h] = total
 
+    small[0].wait()
+    small[1].wait()
+    gain[...] = gain_in[...].astype(F32)
     load_h.wait()
     compute(0)
     compute(1)
@@ -219,7 +225,7 @@
     for k in range(1, ndp):
         wcopies[k].wait_recv()
         weight = weight + wrecv[k, 0:1, :]
-    wmu[...] = wmg[...] + weight / ndp
+    wmu[...] = weight / ndp
 
     for copies in (rcopies, hcopies):
         for copy in copies.values():
@@ -238,7 +244,6 @@
     chunk, rows, no = width // nt, width // ndp, nt // 2
     vmem = pl.BlockSpec(memory_space=pltpu.VMEM)
     anywhere = pl.BlockSpec(memory_space=pl.ANY)
-    hbm = pl.BlockSpec(memory_space=pltpu.HBM)
     dma = pltpu.SemaphoreType.DMA
     piece = chunk // PARTS
     hsg, hg, gg, wmu, gout = pl.pallas_call(
@@ -250,10 +255,12 @@
             jax.ShapeDtypeStruct((1, chunk), F32),
             jax.ShapeDtypeStruct((rows // 128, 128), F32),
         ),
-        in_specs=[hbm, vmem, vmem, hbm, vmem],
+        in_specs=[anywhere] * 4,
         out_specs=(vmem, anywhere, anywhere, vmem, vmem),
         scratch_shapes=[
             pltpu.VMEM((tokens, width), BF16),
+            pltpu.VMEM((width // 128, 128), BF16),
+            pltpu.VMEM((tokens, features), BF16),
             pltpu.VMEM((width // 128, 128), F32),
             pltpu.VMEM((SLOTS, piece, features), BF16),
             pltpu.VMEM((no, PARTS, tokens, piece), F32),
@@ -267,19 +274,19 @@
             pltpu.VMEM((nt, 8, tokens), F32),
             pltpu.VMEM((8, chunk), F32),
             pltpu.VMEM((ndp, 8, chunk), F32),
-            dma((SLOTS,)), dma((3,)),
+            dma((SLOTS,)), dma((5,)),
             dma((no, PARTS)), dma((no, PARTS)), dma((no, PARTS)), dma((no, PARTS)),
             dma((ndp,)), dma((ndp,)), dma((ndp,)), dma((ndp,)),
             dma((nt,)), dma((nt,)), dma((ndp,)), dma((ndp,)),
         ],
         compiler_params=pltpu.CompilerParams(
-            collective_id=0, has_side_effects=True, vmem_limit_bytes=VMEM_MIB * 1024 * 1024),
-    )(hidden_in, norm_gain.reshape(width // 128, 128), q_grad, q_weight, weight_main_gradient.reshape(1, chunk))
+            collective_id=0, has_side_effects=True, vmem_limit_bytes=VMEM_KIB * 1024),
+    )(hidden_in, norm_gain.reshape(width // 128, 128), q_grad, q_weight)
     product = lax.dot_general(
         hg.reshape(ndp * tokens, rows), gg.reshape(ndp * tokens, features),
         (((0,), (0,)), ((), ())), preferred_element_type=F32)
     q_main_new = q_main + product * gout.reshape(rows)[:, None]
-    return hsg, q_main_new, wmu.reshape(chunk)
+    return hsg, q_main_new, weight_main_gradient + wmu.reshape(chunk)
 
 
 def solution(mesh):

time: 56.3 us -> 48 us (0.85)
  local copies, waits for them, and re-layouts: 11 us -> 2.37 us
  other arithmetic: 0 us -> 0.6 us
    unnamed x14 -> x9, local copies, waits for them, and re-layouts: 11 us -> 2.37 us
    add x0 -> x1, other arithmetic: none -> 0.6 us  [body(): return (hsg, q_main_new, weight_main_gradient + wmu.reshape(chunk))]
where the time goes in v3:
time: 48 us; the launch traced here: 47.8 us
  Pallas kernels  38.1 us (79%)
  matrix products  6.07 us (13%)
  local copies, waits for them, and re-layouts  2.37 us (5%)
  between operations  0.66 us (1%)
  other arithmetic  0.6 us (1%)
    pallas_call x1, Pallas kernels, body(): pl.pallas_call(functools.partial(kernel, ndp, nt), out_shape=(jax.ShapeDt...  38.1 us
    dot_general x1, matrix products, body(): lax.dot_general(hg.reshape(ndp * tokens, rows), gg.reshape(ndp * tokens,...  6.07 us
    unnamed x9, local copies, waits for them, and re-layouts  2.37 us

profile of v3, /device:TPU:0, one launch (start us, length us, event | category | flops | bytes accessed | tf_op | source)
XLA Modules:
  0.0 47.8 jit_solution(7625693857399582758)
XLA Ops:
  0.6 0.0 copy-start
  0.6 0.9 %copy-done = bf16[128,1024]{1,0:T(8,128)(2,1)S(1)} copy-done((bf16[128,1024]{1,0:T(8,128)(2,1)S(1)}, bf16[128,1024]{1,0:T(8,128)(2,1)}, u32[]{:S(2)}) %copy-start) | copy-done | bytes 262168
  1.6 0.0 copy-start.1
  1.6 0.7 %copy-done.1 = bf16[8192]{0:T(1024)(128)(2,1)S(1)} copy-done((bf16[8192]{0:T(1024)(128)(2,1)S(1)}, bf16[8192]{0:T(1024)(128)(2,1)}, u32[]{:S(2)}) %copy-start.1) | copy-done | bytes 16408
  2.3 0.0 copy-start.3
  2.3 0.0 copy-start.2
  2.3 38.1 %shard_map.85 = (bf16[128,1024]{1,0:T(8,128)(2,1)S(1)}, bf16[4,128,2048]{2,1,0:T(8,128)(2,1)S(1)}, bf16[4,128,1024]{2,1,0:T(8,128)(2,1)S(1)}, f32[1,1024]{1,0:T(1,128)S(1)}, f32[16,128]{1,0:T(8,128)S(1)}) custom-call(bf16[128,8192]{1,0:T(8,128)(2,1)} %hid_hbm.1, bf16[64,128]{1,0:T(8,128)(2,1)S(1)} %bitcast.10, bf16[128,1024]{1,0:T(8,128)(2,1)S(1)} %copy-done, ...), custom_call_target="tpu_custom_call" | custom-call | tf_op jit(solution)/shard_map/pallas_call | solution.py:249
  40.4 0.0 copy-done.3
  40.4 0.6 %add.7 = f32[1024]{0:T(1024)} add(f32[1024]{0:T(1024)S(1)} %copy-done.3, f32[1024]{0:T(1024)S(1)} %bitcast.11) | non-fusion elementwise | flops 1024 | bytes 12288 | tf_op jit(solution)/shard_map/add | solution.py:289
  41.0 0.0 copy-done.2
  41.0 6.1 %fusion = f32[2048,1024]{1,0:T(8,128)} fusion(f32[2048,1024]{1,0:T(8,128)S(1)} %copy-done.2, bf16[4,128,2048]{2,1,0:T(8,128)(2,1)S(1)} %get-tuple-element.9, bf16[4,128,1024]{2,1,0:T(8,128)(2,1)S(1)} %get-tuple-element.10, f32[2048]{0:T(1024)S(1)} %bitcast.9), kind=kOutput, calls=%fused_computation.1 | convolution fusion | flops 2151677952 | bytes 19931136 | tf_op jit(solution)/shard_map/dot_general | solution.py:285
  47.1 0.7 %copy.12 = bf16[128,1024]{1,0:T(8,128)(2,1)} copy(bf16[128,1024]{1,0:T(8,128)(2,1)S(1)} %get-tuple-element.16) | data formatting | bytes 524288
Async XLA Ops:
  0.6 1.0 %copy-start = (bf16[128,1024]{1,0:T(8,128)(2,1)S(1)}, bf16[128,1024]{1,0:T(8,128)(2,1)}, u32[]{:S(2)}) copy-start(bf16[128,1024]{1,0:T(8,128)(2,1)} %qg_hbm.1) | copy-start | bytes 786436
  1.6 0.7 %copy-start.1 = (bf16[8192]{0:T(1024)(128)(2,1)S(1)}, bf16[8192]{0:T(1024)(128)(2,1)}, u32[]{:S(2)}) copy-start(bf16[8192]{0:T(1024)(128)(2,1)} %param.7) | copy-start | bytes 49156
  2.3 38.1 %copy-start.3 = (f32[1024]{0:T(1024)S(1)}, f32[1024]{0:T(1024)}, u32[]{:S(2)}) copy-start(f32[1024]{0:T(1024)} %param.11) | copy-start | bytes 12292
  2.3 38.7 %copy-start.2 = (f32[2048,1024]{1,0:T(8,128)S(1)}, f32[2048,1024]{1,0:T(8,128)}, u32[]{:S(2)}) copy-start(f32[2048,1024]{1,0:T(8,128)} %param.10) | copy-start | bytes 25165828
